TPU v7x, 32 devices: a whole 2x2x4 slice. The times are simulated.
32 devices in a mesh: len: 2 (over x), tile: 16 (over z, y, core).
Axes of the slice: x: 2, y: 2, z: 4, core: 2. Of those that a mesh axis runs over, the one named last changes fastest.
Arguments:
- series: float32 [9216], P('tile'), may hold values from -24 to 24
- window_lengths: int32 [4], P('len'), may hold values from 64 to 1024, as said below
- exclusion: int32 [4], P('len'), may hold values from 16 to 256
- tile_list: int32 [64, 2], P('tile'), may hold values from 0 to 15, as said below
Outputs:
- right_profile: float32 [4, 8192], P(None, 'tile')
- left_profile: float32 [4, 8192], P(None, 'tile')
Inputs may be any that keep to these rules, and one draw needn't show every extreme that they name: `window_lengths`: the largest is exactly 1024. `tile_list`: each row is a pair (row block, column block) with row block <= column block; no pair appears twice.
All inputs are finite; a program needn't handle non-finite values.
Results may differ from a plain program's by a relative error of at most 0.00039.
Values sent between devices are 32-bit elements; how exact they have to be, the bound alone decides.
No kernel may reach another device: no remote copies, remote signals or barrier semaphores. Data moves between devices by JAX's collectives and lax.ppermute only.
A program may use at most 64 MiB of HBM per device.

v0:
```python
import jax
import jax.numpy as jnp
from jax import lax
from jax.sharding import PartitionSpec as P

MAX_LEN = 1024
TILE_SIDE = 512
COL_BLOCK = 512


EMPTY_VALUE = 2.0
VAR_EPS = 1e-05


def shifted_block(segment, offset, columns, positions):
    window = lax.dynamic_slice_in_dim(segment, offset, positions + columns)
    stride = positions + columns + 1
    repeated = jnp.tile(window, columns + 1)[: columns * stride]
    return repeated.reshape(columns, stride)[:, :positions]


def window_stats(segment, length, positions, columns):
    blocks = (length + columns - 1) // columns
    col_ids = lax.broadcasted_iota(jnp.int32, (columns, 1), 0)
    denominator = length.astype(jnp.float32)
    initial = jnp.zeros((positions,), jnp.float32)

    def add_sum(part_index, running):
        values = shifted_block(segment, part_index * columns, columns, positions)
        inside = col_ids + part_index * columns < length
        return running + jnp.sum(jnp.where(inside, values, 0.0), axis=0)

    centre = lax.fori_loop(0, blocks, add_sum, initial) / denominator

    def add_square(part_index, running):
        values = shifted_block(segment, part_index * columns, columns, positions) - centre[None, :]
        inside = col_ids + part_index * columns < length
        return running + jnp.sum(jnp.where(inside, values * values, 0.0), axis=0)

    spread = lax.fori_loop(0, blocks, add_square, initial) / denominator
    return (centre, 1.0 / jnp.sqrt(spread + VAR_EPS))


def normalized(segment, part_index, centre, inverse, length):
    values = shifted_block(segment, part_index * COL_BLOCK, COL_BLOCK, TILE_SIDE)
    col_ids = lax.broadcasted_iota(jnp.int32, (COL_BLOCK, 1), 0)
    inside = col_ids + part_index * COL_BLOCK < length
    return jnp.where(inside, (values - centre[None, :]) * inverse[None, :], 0.0).astype(
        jnp.bfloat16
    )


def tile_minima(
    row_segment, col_segment, row_stats, col_stats, length, barrier, row_start, col_start, active
):
    blocks = jnp.where(active, (length + COL_BLOCK - 1) // COL_BLOCK, 0)

    def add_block(part_index, running):
        row_normal = normalized(row_segment, part_index, row_stats[0], row_stats[1], length)
        col_normal = normalized(col_segment, part_index, col_stats[0], col_stats[1], length)
        return running + lax.dot_general(
            row_normal, col_normal, (((0,), (0,)), ((), ())), preferred_element_type=jnp.float32
        )

    product = lax.fori_loop(0, blocks, add_block, jnp.zeros((TILE_SIDE, TILE_SIDE), jnp.float32))
    distance = 1.0 - product / length.astype(jnp.float32)
    row_ids = row_start + lax.broadcasted_iota(jnp.int32, (TILE_SIDE, 1), 0)
    col_ids = col_start + lax.broadcasted_iota(jnp.int32, (1, TILE_SIDE), 1)
    allowed = jnp.logical_and(col_ids - row_ids > barrier, active)
    distance = jnp.where(allowed, distance, EMPTY_VALUE)
    return (jnp.min(distance, axis=1), jnp.min(distance, axis=0))


def shared_stats(full_series, lengths):
    time_share = (full_series.shape[0] - MAX_LEN) // lax.axis_size("tile")
    segment = lax.dynamic_slice_in_dim(
        full_series, lax.axis_index("tile") * time_share, time_share + MAX_LEN
    )

    def one_length(length):
        return window_stats(segment, length, time_share, COL_BLOCK)

    centres, inverses = lax.map(one_length, lengths)
    return (
        lax.all_gather(centres, "tile", axis=1, tiled=True),
        lax.all_gather(inverses, "tile", axis=1, tiled=True),
    )


def sweep(full_series, lengths, barriers, tile_slots, alive_slots, stats_all):
    count_len = lengths.shape[0]
    positions = full_series.shape[0] - MAX_LEN
    blank = jnp.full((count_len, positions), EMPTY_VALUE, jnp.float32)

    def per_slot(slot_index, profiles):
        row_start = tile_slots[slot_index, 0] * TILE_SIDE
        col_start = tile_slots[slot_index, 1] * TILE_SIDE
        active = alive_slots[slot_index]
        row_segment = lax.dynamic_slice_in_dim(full_series, row_start, TILE_SIDE + MAX_LEN)
        col_segment = lax.dynamic_slice_in_dim(full_series, col_start, TILE_SIDE + MAX_LEN)

        def per_length(length_index, current):
            right_lowest_distance, left_best = current
            length = lengths[length_index]
            barrier = barriers[length_index]
            row_stats = tuple(
                (
                    lax.dynamic_slice(source, (length_index, row_start), (1, TILE_SIDE))[0]
                    for source in stats_all
                )
            )
            col_stats = tuple(
                (
                    lax.dynamic_slice(source, (length_index, col_start), (1, TILE_SIDE))[0]
                    for source in stats_all
                )
            )
            right_min, left_min = tile_minima(
                row_segment,
                col_segment,
                row_stats,
                col_stats,
                length,
                barrier,
                row_start,
                col_start,
                active,
            )
            right_old = lax.dynamic_slice(
                right_lowest_distance, (length_index, row_start), (1, TILE_SIDE)
            )
            right_lowest_distance = lax.dynamic_update_slice(
                right_lowest_distance,
                jnp.minimum(right_old, right_min[None, :]),
                (length_index, row_start),
            )
            left_old = lax.dynamic_slice(left_best, (length_index, col_start), (1, TILE_SIDE))
            left_best = lax.dynamic_update_slice(
                left_best, jnp.minimum(left_old, left_min[None, :]), (length_index, col_start)
            )
            return (right_lowest_distance, left_best)

        return lax.fori_loop(0, count_len, per_length, profiles)

    return lax.fori_loop(0, tile_slots.shape[0], per_slot, (blank, blank))


def merge_tile(right_lowest_distance, left_best):
    count_tile = lax.axis_size("tile")
    rows_len, positions = right_lowest_distance.shape
    time_share = positions // count_tile
    right_parts, left_parts = (
        lax.all_to_all(
            right_lowest_distance.reshape(rows_len, count_tile, time_share),
            "tile",
            split_axis=1,
            concat_axis=1,
            tiled=True,
        ),
        lax.all_to_all(
            left_best.reshape(rows_len, count_tile, time_share),
            "tile",
            split_axis=1,
            concat_axis=1,
            tiled=True,
        ),
    )
    merged = (jnp.min(right_parts, axis=1), jnp.min(left_parts, axis=1))
    return merged


def shards(series, window_lengths, exclusion, tile_list):
    full_series = lax.all_gather(series, "tile", axis=0, tiled=True)
    lengths, barriers = (window_lengths, exclusion)
    alive_slots = jnp.ones((tile_list.shape[0],), jnp.bool_)
    stats_all = shared_stats(full_series, lengths)
    right_lowest_distance, left_best = sweep(
        full_series, lengths, barriers, tile_list, alive_slots, stats_all
    )
    right_lowest_distance, left_best = merge_tile(right_lowest_distance, left_best)
    right_lowest_distance, left_best = (
        lax.all_gather(right_lowest_distance, "len", axis=0, tiled=True),
        lax.all_gather(left_best, "len", axis=0, tiled=True),
    )
    return (right_lowest_distance, left_best)


def solution(mesh):
    return jax.shard_map(
        shards,
        mesh=mesh,
        in_specs=(P("tile"), P("len"), P("len"), P("tile", None)),
        out_specs=(P(None, "tile"), P(None, "tile")),
        check_vma=False,
    )
```

profile of v0, /device:TPU:12, one launch (start us, length us, event | category | flops | bytes accessed | tf_op | source)
XLA Modules:
  0.0 426.9 jit_solution(2934008944856751509)
XLA Ops:
  3.5 49.0 %all-reduce = f32[9216]{0:T(1024)S(1)} all-reduce(f32[9216]{0:T(1024)S(1)} %dynamic-update-slice), channel_id=1, replica_groups=mesh['len'=2,'tile'=16] {'tile'}, use_global_device_ids=true, to_apply=%add | all-reduce | flops 9216 | bytes 73728
  53.1 41.6 %while.171 = (s32[]{:T(128)}, f32[2,512]{1,0:T(2,128)S(1)}, f32[2,512]{1,0:T(2,128)S(1)}, s32[2]{0:T(128)}, f32[1536]{0:T(1024)S(1)}, /*index=5*/s32[]{:T(128)},...) while((s32[]{:T(128)}, f32[2,512]{1,0:T(2,128)S(1)}, ...), condition=%wide.region_7.8_spmd, body=%wide.region_0.7_spmd.sunk | while | flops 1576479 | bytes 23167832 | solution.py:83
  55.0 6.0 %while.174 = (s32[]{:T(128)}, f32[512]{0:T(512)S(1)}, s32[]{:T(128)}, s32[]{:T(128)}, f32[1536]{0:T(1024)S(1)}, /*index=5*/s32[]{:T(128)}, s32[]{:T(128)}, s32[]{:T(128)}, s32[]{:T(128)}) while((s32[]{:T(128)}, f32[512]{0:T(512)S(1)}, s32[]{:T(128)}, s32[]{:T(128)}, f32[1536]{0:T(1024)S(1)}, /*index=5*/s32[]{:T(128)}, s32[]{:T(128)}, ...), condition=%wide.region_3.3_spmd.clone, body=%wide.region_1.2_spmd.clone.sunk | while | flops 525318 | bytes 11572375 | solution.py:33
  61.7 6.0 %while.175 = (s32[]{:T(128)}, f32[512]{0:T(512)S(1)}, s32[]{:T(128)}, s32[]{:T(128)}, f32[1536]{0:T(1024)S(1)}, /*index=5*/f32[512]{0:T(512)S(1)}, s32[]{:T(128)}, s32[]{:T(128)}, s32[]{:T(128)}, s32[]{:T(128)}) while((s32[]{:T(128)}, f32[512]{0:T(512)S(1)}, s32[]{:T(128)}, s32[]{:T(128)}, f32[1536]{0:T(1024)S(1)}, ...), condition=%wide.region_6.6_spmd.clone, body=%wide.region_4.5_spmd.clone.sunk | while | flops 1049606 | bytes 11574431 | solution.py:40
  69.8 12.1 %while.174 = (s32[]{:T(128)}, f32[512]{0:T(512)S(1)}, s32[]{:T(128)}, s32[]{:T(128)}, f32[1536]{0:T(1024)S(1)}, /*index=5*/s32[]{:T(128)}, s32[]{:T(128)}, s32[]{:T(128)}, s32[]{:T(128)}) while((s32[]{:T(128)}, f32[512]{0:T(512)S(1)}, s32[]{:T(128)}, s32[]{:T(128)}, f32[1536]{0:T(1024)S(1)}, /*index=5*/s32[]{:T(128)}, s32[]{:T(128)}, ...), condition=%wide.region_3.3_spmd.clone, body=%wide.region_1.2_spmd.clone.sunk | while | flops 525318 | bytes 11572375 | solution.py:33
  82.5 12.1 %while.175 = (s32[]{:T(128)}, f32[512]{0:T(512)S(1)}, s32[]{:T(128)}, s32[]{:T(128)}, f32[1536]{0:T(1024)S(1)}, /*index=5*/f32[512]{0:T(512)S(1)}, s32[]{:T(128)}, s32[]{:T(128)}, s32[]{:T(128)}, s32[]{:T(128)}) while((s32[]{:T(128)}, f32[512]{0:T(512)S(1)}, s32[]{:T(128)}, s32[]{:T(128)}, f32[1536]{0:T(1024)S(1)}, ...), condition=%wide.region_6.6_spmd.clone, body=%wide.region_4.5_spmd.clone.sunk | while | flops 1049606 | bytes 11574431 | solution.py:40
  94.7 27.4 %all_gather.16 = f32[2,8192]{1,0:T(2,128)S(1)} all-gather(f32[2,512]{1,0:T(2,128)S(1)} %get-tuple-element.1002), channel_id=1, replica_groups=mesh['len'=2,'tile'=16] {'tile'}, dimensions={1}, use_global_device_ids=true | all-gather | bytes 69632 | tf_op jit(solution)/shard_map/all_gather | solution.py:85
  122.1 18.7 %all_gather.17 = f32[2,8192]{1,0:T(2,128)} all-gather(f32[2,512]{1,0:T(2,128)S(1)} %get-tuple-element.1003), channel_id=1, replica_groups=mesh['len'=2,'tile'=16] {'tile'}, dimensions={1}, use_global_device_ids=true | all-gather | bytes 69632 | tf_op jit(solution)/shard_map/all_gather | solution.py:86
  142.1 256.4 %while.173 = (s32[]{:T(128)}, f32[2,8192]{1,0:T(2,128)}, f32[2,8192]{1,0:T(2,128)}, s32[4,2]{0,1:T(2,128)}, f32[9216]{0:T(1024)}, /*index=5*/s32[2]{0:T(128)}, s...) while((s32[]{:T(128)}, f32[2,8192]{1,0:T(2,128)}, ...), condition=%wide.region_15.16_spmd, body=%wide.region_8.15_spmd.sunk | while | flops 272631840 | bytes 27405192 | solution.py:145
  145.6 60.5 %while.176 = (s32[]{:T(128)}, f32[2,8192]{1,0:T(2,128)}, f32[2,8192]{1,0:T(2,128)}, s32[]{:T(128)}, s32[]{:T(128)}, /*index=5*/s32[]{:T(128)}, s32[2]{0:T(128)},...) while((s32[]{:T(128)}, f32[2,8192]{1,0:T(2,128)}, ...), condition=%wide.region_14.14_spmd, body=%wide.region_9.13_spmd.sunk | while | flops 272631840 | bytes 27380040 | solution.py:143
  148.6 14.3 %while.177 = (s32[]{:T(128)}, f32[512,512]{1,0:T(8,128)S(1)}, s32[]{:T(128)}, s32[]{:T(128)}, f32[1536]{0:T(1024)S(1)}, /*index=5*/f32[1,512]{1,0:T(1,128)S(1)},...) while((s32[]{:T(128)}, f32[512,512]{1,0:T(8,128)S(1)}, ...), condition=%wide.region_11.10_spmd, body=%wide.region_10.9_spmd.sunk | while | flops 270795776 | bytes 25233092 | solution.py:65
  150.6 4.6 %reshape.89 = f32[512,1025]{1,0:T(8,128)} reshape(f32[524800]{0:T(1024)} %bitcast.56) | data formatting | bytes 4198400 | tf_op jit(solution)/shard_map/while/body/eval_jaxpr/while/body/eval_jaxpr/while/body/reshape | solution.py:19
  171.7 28.6 %while.177 = (s32[]{:T(128)}, f32[512,512]{1,0:T(8,128)S(1)}, s32[]{:T(128)}, s32[]{:T(128)}, f32[1536]{0:T(1024)S(1)}, /*index=5*/f32[1,512]{1,0:T(1,128)S(1)},...) while((s32[]{:T(128)}, f32[512,512]{1,0:T(8,128)S(1)}, ...), condition=%wide.region_11.10_spmd, body=%wide.region_10.9_spmd.sunk | while | flops 270795776 | bytes 25233092 | solution.py:65
  209.8 60.5 %while.176 = (s32[]{:T(128)}, f32[2,8192]{1,0:T(2,128)}, f32[2,8192]{1,0:T(2,128)}, s32[]{:T(128)}, s32[]{:T(128)}, /*index=5*/s32[]{:T(128)}, s32[2]{0:T(128)},...) while((s32[]{:T(128)}, f32[2,8192]{1,0:T(2,128)}, ...), condition=%wide.region_14.14_spmd, body=%wide.region_9.13_spmd.sunk | while | flops 272631840 | bytes 27380040 | solution.py:143
  212.7 14.3 %while.177 = (s32[]{:T(128)}, f32[512,512]{1,0:T(8,128)S(1)}, s32[]{:T(128)}, s32[]{:T(128)}, f32[1536]{0:T(1024)S(1)}, /*index=5*/f32[1,512]{1,0:T(1,128)S(1)},...) while((s32[]{:T(128)}, f32[512,512]{1,0:T(8,128)S(1)}, ...), condition=%wide.region_11.10_spmd, body=%wide.region_10.9_spmd.sunk | while | flops 270795776 | bytes 25233092 | solution.py:65
  235.8 28.6 %while.177 = (s32[]{:T(128)}, f32[512,512]{1,0:T(8,128)S(1)}, s32[]{:T(128)}, s32[]{:T(128)}, f32[1536]{0:T(1024)S(1)}, /*index=5*/f32[1,512]{1,0:T(1,128)S(1)},...) while((s32[]{:T(128)}, f32[512,512]{1,0:T(8,128)S(1)}, ...), condition=%wide.region_11.10_spmd, body=%wide.region_10.9_spmd.sunk | while | flops 270795776 | bytes 25233092 | solution.py:65
  273.8 60.5 %while.176 = (s32[]{:T(128)}, f32[2,8192]{1,0:T(2,128)}, f32[2,8192]{1,0:T(2,128)}, s32[]{:T(128)}, s32[]{:T(128)}, /*index=5*/s32[]{:T(128)}, s32[2]{0:T(128)},...) while((s32[]{:T(128)}, f32[2,8192]{1,0:T(2,128)}, ...), condition=%wide.region_14.14_spmd, body=%wide.region_9.13_spmd.sunk | while | flops 272631840 | bytes 27380040 | solution.py:143
  276.7 14.3 %while.177 = (s32[]{:T(128)}, f32[512,512]{1,0:T(8,128)S(1)}, s32[]{:T(128)}, s32[]{:T(128)}, f32[1536]{0:T(1024)S(1)}, /*index=5*/f32[1,512]{1,0:T(1,128)S(1)},...) while((s32[]{:T(128)}, f32[512,512]{1,0:T(8,128)S(1)}, ...), condition=%wide.region_11.10_spmd, body=%wide.region_10.9_spmd.sunk | while | flops 270795776 | bytes 25233092 | solution.py:65
  299.9 28.6 %while.177 = (s32[]{:T(128)}, f32[512,512]{1,0:T(8,128)S(1)}, s32[]{:T(128)}, s32[]{:T(128)}, f32[1536]{0:T(1024)S(1)}, /*index=5*/f32[1,512]{1,0:T(1,128)S(1)},...) while((s32[]{:T(128)}, f32[512,512]{1,0:T(8,128)S(1)}, ...), condition=%wide.region_11.10_spmd, body=%wide.region_10.9_spmd.sunk | while | flops 270795776 | bytes 25233092 | solution.py:65
  338.0 60.5 %while.176 = (s32[]{:T(128)}, f32[2,8192]{1,0:T(2,128)}, f32[2,8192]{1,0:T(2,128)}, s32[]{:T(128)}, s32[]{:T(128)}, /*index=5*/s32[]{:T(128)}, s32[2]{0:T(128)},...) while((s32[]{:T(128)}, f32[2,8192]{1,0:T(2,128)}, ...), condition=%wide.region_14.14_spmd, body=%wide.region_9.13_spmd.sunk | while | flops 272631840 | bytes 27380040 | solution.py:143
  340.9 14.3 %while.177 = (s32[]{:T(128)}, f32[512,512]{1,0:T(8,128)S(1)}, s32[]{:T(128)}, s32[]{:T(128)}, f32[1536]{0:T(1024)S(1)}, /*index=5*/f32[1,512]{1,0:T(1,128)S(1)},...) while((s32[]{:T(128)}, f32[512,512]{1,0:T(8,128)S(1)}, ...), condition=%wide.region_11.10_spmd, body=%wide.region_10.9_spmd.sunk | while | flops 270795776 | bytes 25233092 | solution.py:65
  364.0 28.6 %while.177 = (s32[]{:T(128)}, f32[512,512]{1,0:T(8,128)S(1)}, s32[]{:T(128)}, s32[]{:T(128)}, f32[1536]{0:T(1024)S(1)}, /*index=5*/f32[1,512]{1,0:T(1,128)S(1)},...) while((s32[]{:T(128)}, f32[512,512]{1,0:T(8,128)S(1)}, ...), condition=%wide.region_11.10_spmd, body=%wide.region_10.9_spmd.sunk | while | flops 270795776 | bytes 25233092 | solution.py:65
  398.5 12.4 %all_to_all.10 = f32[2,16,512]{2,0,1:T(2,128)S(1)} all-to-all(f32[2,16,512]{2,0,1:T(2,128)} %bitcast.67), channel_id=1, replica_groups=mesh['len'=2,'tile'=16] {'tile'}, dimensions={1} | all-to-all | bytes 131072 | tf_op jit(solution)/shard_map/all_to_all | solution.py:153
  410.9 6.0 %all-to-all-start.1 = ((f32[2,16,512]{2,0,1:T(2,128)}), f32[2,16,512]{2,0,1:T(2,128)S(1)}, u32[]{:S(2)}, u32[]{:S(2)}) async-start(f32[2,16,512]{2,0,1:T(2,128)} %bitcast.68), calls=%async_computation.1 | async-start | bytes 131072 | tf_op jit(solution)/shard_map/all_to_all | solution.py:160
  (304 shorter events, 287.7 us)
Async XLA Ops:
  52.5 0.6 copy-start
  148.6 15.0 %copy-start.1 = (s32[2]{0:T(128)S(1)}, s32[2]{0:T(128)}, u32[]{:S(2)}) copy-start(s32[2]{0:T(128)} %get-tuple-element.1638) | copy-start | bytes 28 | tf_op jit(solution)/shard_map/while/body/eval_jaxpr/while
  171.6 29.3 %copy-start.1 = (s32[2]{0:T(128)S(1)}, s32[2]{0:T(128)}, u32[]{:S(2)}) copy-start(s32[2]{0:T(128)} %get-tuple-element.1638) | copy-start | bytes 28 | tf_op jit(solution)/shard_map/while/body/eval_jaxpr/while
  212.7 15.0 %copy-start.1 = (s32[2]{0:T(128)S(1)}, s32[2]{0:T(128)}, u32[]{:S(2)}) copy-start(s32[2]{0:T(128)} %get-tuple-element.1638) | copy-start | bytes 28 | tf_op jit(solution)/shard_map/while/body/eval_jaxpr/while
  235.8 29.3 %copy-start.1 = (s32[2]{0:T(128)S(1)}, s32[2]{0:T(128)}, u32[]{:S(2)}) copy-start(s32[2]{0:T(128)} %get-tuple-element.1638) | copy-start | bytes 28 | tf_op jit(solution)/shard_map/while/body/eval_jaxpr/while
  276.7 15.0 %copy-start.1 = (s32[2]{0:T(128)S(1)}, s32[2]{0:T(128)}, u32[]{:S(2)}) copy-start(s32[2]{0:T(128)} %get-tuple-element.1638) | copy-start | bytes 28 | tf_op jit(solution)/shard_map/while/body/eval_jaxpr/while
  299.8 29.3 %copy-start.1 = (s32[2]{0:T(128)S(1)}, s32[2]{0:T(128)}, u32[]{:S(2)}) copy-start(s32[2]{0:T(128)} %get-tuple-element.1638) | copy-start | bytes 28 | tf_op jit(solution)/shard_map/while/body/eval_jaxpr/while
  340.9 15.0 %copy-start.1 = (s32[2]{0:T(128)S(1)}, s32[2]{0:T(128)}, u32[]{:S(2)}) copy-start(s32[2]{0:T(128)} %get-tuple-element.1638) | copy-start | bytes 28 | tf_op jit(solution)/shard_map/while/body/eval_jaxpr/while
  364.0 29.3 %copy-start.1 = (s32[2]{0:T(128)S(1)}, s32[2]{0:T(128)}, u32[]{:S(2)}) copy-start(s32[2]{0:T(128)} %get-tuple-element.1638) | copy-start | bytes 28 | tf_op jit(solution)/shard_map/while/body/eval_jaxpr/while
  410.9 11.0 %all-to-all-start.1 = ((f32[2,16,512]{2,0,1:T(2,128)}), f32[2,16,512]{2,0,1:T(2,128)S(1)}, u32[]{:S(2)}, u32[]{:S(2)}) async-start(f32[2,16,512]{2,0,1:T(2,128)} %bitcast.68), calls=%async_computation.1 | async-start | bytes 131072 | tf_op jit(solution)/shard_map/all_to_all | solution.py:160
where the time goes:
time: 434 us; the launch traced here: 427 us
  local copies, waits for them, and re-layouts  234 us (54%)
  blocking collectives  116 us (27%)
  other arithmetic  27.3 us (6%)
  matrix products  22.6 us (5%)
  loops' own time  19.7 us (5%)
  starting transfers between devices  6.04 us (1%)
    reshape x30, local copies, waits for them, and re-layouts, shifted_block(): return repeated.reshape(columns, stride)[:, :positions]  112 us
    another operation x60, local copies, waits for them, and re-layouts, shifted_block(): repeated = jnp.tile(window, columns + 1)[:columns * stride]  57.1 us
    unnamed x1, blocking collectives  49 us
    all_gather x1, blocking collectives, shared_stats(): lax.all_gather(centres, 'tile', axis=1, tiled=True)  27.4 us
    dot_general x12, matrix products, add_block(): lax.dot_general(row_normal, col_normal, (((0,), (0,)), ((), ())), preferr...  22.6 us
    all_gather x1, blocking collectives, shared_stats(): lax.all_gather(inverses, 'tile', axis=1, tiled=True)  18.7 us
    all_to_all x1, blocking collectives, merge_tile(): lax.all_to_all(right_lowest_distance.reshape(rows_len, count_tile, time_s...  12.4 us
    dynamic_update_slice x8, local copies, waits for them, and re-layouts, per_length(): lax.dynamic_update_slice(left_best, jnp.minimum(left_old, left_min[None,...  10.7 us
  transfers between devices with their start and end apart: 1, of which 0 were waited for; matrix products, arithmetic and copies ran while one was open for 0% of the time, Pallas kernels for 0%

commit v1 on v0

v1 whole, which is shorter than its diff:
```python
import functools

import jax
import jax.numpy as jnp
from jax import lax
from jax.experimental import pallas as pl
from jax.experimental.pallas import tpu as pltpu
from jax.sharding import PartitionSpec as P

MAX_LEN = 1024
TILE_SIDE = 512
EMPTY_VALUE = 2.0
VAR_EPS = 1e-05
LANES = 128
CHUNK = 256
LOWEST = -3.0e38
WORD = 16


def round_up(value, multiple):
    return (value + multiple - 1) // multiple * multiple


def packed_piece(series, window_lengths, exclusion, tile_list):
    piece_rows = -(-series.shape[0] // LANES)
    rows = round_up(piece_rows + 3, 8)
    values = jnp.pad(series, (0, piece_rows * LANES - series.shape[0])).reshape(piece_rows, LANES)
    slots = tile_list.astype(jnp.float32).T
    slots = jnp.pad(slots, ((0, 0), (0, LANES - slots.shape[1])), constant_values=-1.0)
    half = LANES // 2
    count = window_lengths.shape[0]
    settings = jnp.concatenate(
        [
            jnp.pad(window_lengths.astype(jnp.float32), (0, half - count)),
            jnp.pad(exclusion.astype(jnp.float32), (0, half - count)),
        ]
    ).reshape(1, LANES)
    spare = jnp.zeros((rows - piece_rows - 3, LANES), jnp.float32)
    return jnp.concatenate([values, slots, settings, spare], axis=0)


def gather_pieces(piece, count_tile, count_len):
    held = piece[None]
    mask = 1
    while mask < count_tile:
        if mask == 2:
            pairs = [
                (a * count_tile + b, (a ^ 1) * count_tile + (b ^ mask))
                for a in range(count_len)
                for b in range(count_tile)
            ]
            other = lax.ppermute(held, ("len", "tile"), pairs)
        else:
            other = lax.ppermute(held, "tile", [(b, b ^ mask) for b in range(count_tile)])
        mask *= 2
        if mask == count_tile:
            return held, other
        held = jnp.concatenate([held, other], axis=0)


def flat_shift(values, amount):
    rows = values.shape[0]
    whole, part = divmod(amount, LANES)
    if whole:
        values = pltpu.roll(values, (rows - whole) % rows, 0)
    if part:
        rolled = pltpu.roll(values, LANES - part, 1)
        following = pltpu.roll(rolled, rows - 1, 0)
        lane = lax.broadcasted_iota(jnp.int32, values.shape, 1)
        values = jnp.where(lane < LANES - part, rolled, following)
    return values


def kernel(
    count_tile,
    count_len,
    count_own,
    piece_length,
    first_ref,
    second_ref,
    out_ref,
    slots_ref,
    flat_ref,
    sum_ref,
    square_ref,
    shifted_ref,
    turned_ref,
    left_ref,
    right_ref,
    best_ref,
    number_ref,
    item_ref,
):
    me = lax.axis_index("tile")
    side = lax.rem(lax.axis_index("len"), 2)
    count = 2 * count_own
    half_slots = count_tile // 2
    piece_rows = -(-piece_length // LANES)
    series_rows = flat_ref.shape[0]
    blocks = TILE_SIDE // LANES
    lane_row = lax.broadcasted_iota(jnp.int32, (1, LANES), 1)

    slots_ref[:half_slots] = first_ref[...]
    slots_ref[half_slots:] = second_ref[...]

    for index in range(count):
        from_own = (index // count_own) == side
        slot = jnp.where(from_own, 0, 2)
        row = slots_ref[slot, pl.ds(piece_rows + 2, 1), :]
        for kind in range(2):
            spot = index % count_own + kind * (LANES // 2)
            number_ref[kind, index] = jnp.sum(jnp.where(lane_row == spot, row, 0.0)).astype(jnp.int32)
    row_ids = slots_ref[:, piece_rows, :].astype(jnp.int32)
    col_ids = slots_ref[:, piece_rows + 1, :].astype(jnp.int32)
    words = -(-count_tile // WORD)
    for kind, (fixed, listed) in enumerate(((row_ids, col_ids), (col_ids, row_ids))):
        for word in range(words):
            spot = listed - word * WORD
            chosen = (fixed == me) & (spot >= 0) & (spot < WORD)
            bit = jnp.left_shift(1, jnp.where(chosen, spot, 0)).astype(jnp.float32)
            number_ref[2 + kind, word] = jnp.sum(jnp.where(chosen, bit, 0.0)).astype(jnp.int32)

    def list_items(kind, start):
        def step(block, carry):
            filled, seen = carry
            present = lax.rem(lax.shift_right_logical(number_ref[2 + kind, block // WORD], lax.rem(block, WORD)), 2)
            odd = lax.rem(seen + side, 2)
            for pair in range(count // 2):
                item_ref[filled] = ((kind * count + 2 * pair + odd) * count_tile) + block
                filled = filled + present
            return filled, seen + present

        return lax.fori_loop(0, count_tile, step, start)

    filled, _ = list_items(1, list_items(0, (jnp.int32(0), jnp.int32(0))))

    flat_ref[...] = jnp.zeros_like(flat_ref)
    lane = lax.broadcasted_iota(jnp.int32, (piece_rows, LANES), 1)
    for index in range(count_tile):
        piece = slots_ref[lax.bitwise_xor(me, index), :piece_rows, :]
        row, offset = divmod(index * piece_length, LANES)
        if offset:
            piece = pltpu.roll(piece, offset, 1)
            flat_ref[row + 1 : row + 1 + piece_rows] += jnp.where(lane < offset, piece, 0.0)
            piece = jnp.where(lane < offset, 0.0, piece)
        flat_ref[row : row + piece_rows] += piece

    for index in range(count):
        sum_ref[index] = jnp.zeros((series_rows, LANES), jnp.float32)
        square_ref[index] = jnp.zeros((series_rows, LANES), jnp.float32)
    level_sum = flat_ref[...]
    level_square = jnp.zeros_like(level_sum)
    size = 1
    while True:
        for index in range(count):
            length = number_ref[0, index]

            @pl.when(lax.bitwise_and(length, size) != 0)
            def _(index=index, length=length, size=size, level_sum=level_sum, level_square=level_square):
                tail = jnp.full((1, 1), lax.bitwise_and(length, size - 1), jnp.int32).astype(jnp.float32)
                tail_sum = flat_shift(sum_ref[index], size)
                tail_square = flat_shift(square_ref[index], size)
                apart = tail_sum * (1.0 / jnp.maximum(tail, 1.0)) - level_sum * (1.0 / size)
                weight = tail * size / (tail + size)
                sum_ref[index] = level_sum + tail_sum
                square_ref[index] = level_square + tail_square + apart * apart * weight

        if size >= MAX_LEN:
            break
        next_sum = flat_shift(level_sum, size)
        next_square = flat_shift(level_square, size)
        apart = (next_sum - level_sum) * (1.0 / size)
        level_sum = level_sum + next_sum
        level_square = level_square + next_square + apart * apart * (size / 2)
        size *= 2
    for index in range(count):
        length = jnp.full((1, 1), number_ref[0, index], jnp.int32).astype(jnp.float32)
        sum_ref[index] = sum_ref[index] / length
        square_ref[index] = 1.0 / jnp.sqrt(square_ref[index] / length + VAR_EPS)

    square_row = lax.broadcasted_iota(jnp.int32, (LANES, LANES), 0)
    square_lane = lax.broadcasted_iota(jnp.int32, (LANES, LANES), 1)
    inside = square_lane <= square_row

    def rotated(row):
        values = jnp.broadcast_to(flat_ref[pl.ds(row, 1), :], (LANES, LANES))
        return pltpu.roll(values, 1, 1, stride=1, stride_axis=0)

    def shift_row(row, current):
        following = rotated(row + 1)
        shifted_ref[row] = jnp.where(inside, current, following)
        return following

    lax.fori_loop(0, series_rows - 1, shift_row, rotated(0))

    best_ref[...] = jnp.full_like(best_ref, LOWEST)
    for spot in range(blocks + MAX_LEN // LANES - 1):
        turned_ref[spot] = shifted_ref[me * blocks + spot].T
    for index in range(count):
        length = number_ref[0, index]
        chunks = (length + CHUNK - 1) // CHUNK
        for block in range(blocks):
            row = me * blocks + block
            centre = jnp.broadcast_to(sum_ref[index, pl.ds(row, 1), :], (LANES, LANES)).T
            inverse = jnp.broadcast_to(square_ref[index, pl.ds(row, 1), :], (LANES, LANES)).T
            for chunk in range(MAX_LEN // CHUNK):

                @pl.when(chunk < chunks)
                def _(index=index, block=block, chunk=chunk, centre=centre, inverse=inverse, length=length):
                    for part in range(CHUNK // LANES):
                        spot = chunk * (CHUNK // LANES) + part
                        values = (turned_ref[block + spot] - centre) * inverse
                        values = jnp.where(LANES - 1 - square_lane < length - spot * LANES, values, 0.0)
                        left_ref[
                            index, block * LANES : (block + 1) * LANES, spot * LANES : (spot + 1) * LANES
                        ] = values.astype(jnp.bfloat16)

    def one_item(position, carry):
        item = item_ref[position]
        other = lax.rem(item, count_tile)
        target = item // count_tile
        kind = target // count
        index = lax.rem(target, count)
        length = number_ref[0, index]
        barrier = number_ref[1, index]
        chunks = (length + CHUNK - 1) // CHUNK
        ahead = jnp.where(kind == 0, 1, -1)
        gap = ahead * (other - me) * TILE_SIDE
        near = gap - (TILE_SIDE - 1) <= barrier

        for steps in range(1, MAX_LEN // CHUNK + 1):
            for masked in (False, True):

                @pl.when((chunks == steps) & (near == masked))
                def _(steps=steps, masked=masked):
                    for block in range(blocks):
                        row = other * blocks + block
                        centre = sum_ref[index, pl.ds(row, 1), :]
                        inverse = square_ref[index, pl.ds(row, 1), :]
                        for spot in range(steps * (CHUNK // LANES)):
                            values = (shifted_ref[row + spot] - centre) * inverse
                            right_ref[
                                spot * LANES : (spot + 1) * LANES, block * LANES : (block + 1) * LANES
                            ] = values.astype(jnp.bfloat16)
                    depth = steps * CHUNK
                    product = jnp.dot(
                        left_ref[index, :, :depth], right_ref[:depth, :], preferred_element_type=jnp.float32
                    )
                    if masked:
                        own_ids = lax.broadcasted_iota(jnp.int32, product.shape, 0)
                        other_ids = lax.broadcasted_iota(jnp.int32, product.shape, 1)
                        product = jnp.where(gap + ahead * (other_ids - own_ids) > barrier, product, LOWEST)
                    best = best_ref[target]
                    for block in range(blocks):
                        best = jnp.maximum(best, product[:, block * LANES : (block + 1) * LANES])
                    best_ref[target] = best

        return carry

    lax.fori_loop(0, filled, one_item, jnp.int32(0))

    for target in range(2 * count):
        length = jnp.full((1, 1), number_ref[0, target % count], jnp.int32).astype(jnp.float32)
        for block in range(blocks):
            best = best_ref[target, block * LANES : (block + 1) * LANES, :].T
            best = jnp.max(best, axis=0, keepdims=True)
            out_ref[target : target + 1, block * LANES : (block + 1) * LANES] = jnp.minimum(
                1.0 - best / length, EMPTY_VALUE
            )


def local_profiles(first, second, count_tile, count_len, count_own, piece_length):
    count = 2 * count_own
    series_rows = round_up(count_tile * piece_length, 8 * LANES) // LANES + 8
    slots = (count_tile,) + first.shape[1:]
    return pl.pallas_call(
        functools.partial(kernel, count_tile, count_len, count_own, piece_length),
        out_shape=jax.ShapeDtypeStruct((2 * count, TILE_SIDE), jnp.float32),
        in_specs=[pl.BlockSpec(memory_space=pltpu.VMEM)] * 2,
        out_specs=pl.BlockSpec(memory_space=pltpu.VMEM),
        scratch_shapes=[
            pltpu.VMEM(slots, jnp.float32),
            pltpu.VMEM((series_rows, LANES), jnp.float32),
            pltpu.VMEM((count, series_rows, LANES), jnp.float32),
            pltpu.VMEM((count, series_rows, LANES), jnp.float32),
            pltpu.VMEM((series_rows, LANES, LANES), jnp.float32),
            pltpu.VMEM(((TILE_SIDE + MAX_LEN) // LANES - 1, LANES, LANES), jnp.float32),
            pltpu.VMEM((count, TILE_SIDE, MAX_LEN), jnp.bfloat16),
            pltpu.VMEM((MAX_LEN, TILE_SIDE), jnp.bfloat16),
            pltpu.VMEM((2 * count, TILE_SIDE, LANES), jnp.float32),
            pltpu.SMEM((4, max(count, -(-count_tile // WORD))), jnp.int32),
            pltpu.SMEM((2 * count_tile * count + count,), jnp.int32),
        ],
        compiler_params=pltpu.CompilerParams(vmem_limit_bytes=56 * 2**20),
        name="profiles",
    )(first, second)


def shards(series, window_lengths, exclusion, tile_list):
    count_tile, count_len = lax.axis_size("tile"), lax.axis_size("len")
    count_own = window_lengths.shape[0]
    piece = packed_piece(series, window_lengths, exclusion, tile_list)
    first, second = gather_pieces(piece, count_tile, count_len)
    local = local_profiles(first, second, count_tile, count_len, count_own, series.shape[0])
    merged = jnp.minimum(local, lax.ppermute(local, "len", [(a, a ^ 1) for a in range(count_len)]))
    merged = merged.reshape(2, 2 * count_own, TILE_SIDE)
    if count_len > 2:
        groups = [list(range(a, count_len, 2)) for a in range(2)]
        merged = lax.all_gather(merged, "len", axis=1, tiled=True, axis_index_groups=groups)
    return merged[0], merged[1]


def solution(mesh):
    return jax.shard_map(
        shards,
        mesh=mesh,
        in_specs=(P("tile"), P("len"), P("len"), P("tile", None)),
        out_specs=(P(None, "tile"), P(None, "tile")),
        check_vma=False,
    )
```

time: 434 us -> 51 us (0.12); the launches traced: 427 us -> 50.1 us
  local copies, waits for them, and re-layouts: 234 us -> 1.22 us
  blocking collectives: 116 us -> 0 us
  Pallas kernels: 0 us -> 27.8 us
  other arithmetic: 27.3 us -> 2.17 us
  matrix products: 22.6 us -> 0 us
  loops' own time: 19.7 us -> 0 us
  waiting for transfers between devices: 0.01 us -> 12.3 us
    reshape x30 -> x1, local copies, waits for them, and re-layouts: 112 us -> 0.01 us  [packed_piece(): jnp.pad(series, (0, piece_rows * LANES - series.shape[0]))]
    another operation x72 -> x0, local copies, waits for them, and re-layouts: 58.1 us -> none  [the longest x60 57.1 us: shifted_block(): repeated = jnp.tile(window, columns + 1)[:columns * stride]]
    all_gather x4 -> x0, blocking collectives: 54.8 us -> none  [the longest x1 27.4 us: shared_stats(): lax.all_gather(centres, 'tile', axis=1, tiled=True)]
    unnamed x1 -> x0, blocking collectives: 49 us -> none
    dynamic_slice x73 -> x0, local copies, waits for them, and re-layouts: 36.4 us -> none  [the longest x8 10.3 us: per_length(): length = lengths[length_index]]
    pallas_call x0 -> x1, Pallas kernels: none -> 27.8 us  [local_profiles(): pl.pallas_call(functools.partial(kernel, count_tile, count_len, count_own...]
    dot_general x12 -> x0, matrix products: 22.6 us -> none  [add_block(): lax.dot_general(row_normal, col_normal, (((0,), (0,)), ((), ())), preferr...]
    dynamic_update_slice x20 -> x0, local copies, waits for them, and re-layouts: 21.6 us -> none  [the longest x8 10.7 us: per_length(): lax.dynamic_update_slice(left_best, jnp.minimum(left_old, left_min[None,...]
  transfers between devices with their start and end apart: 1 -> 5, of which waited for: 0 -> 5; matrix products, arithmetic and copies ran while one was open for 0% -> 0% of each run, Pallas kernels for 0% -> 0%
where the time goes in v1:
time: 51 us; the launch traced here: 50.1 us
  Pallas kernels  27.8 us (55%)
  waiting for transfers between devices  12.3 us (24%)
  starting transfers between devices  6.02 us (12%)
  other arithmetic  2.17 us (4%)
  local copies, waits for them, and re-layouts  1.22 us (2%)
  between operations  0.67 us (1%)
    pallas_call x1, Pallas kernels, local_profiles(): pl.pallas_call(functools.partial(kernel, count_tile, count_len, count_own...  27.8 us
    ppermute x3, waiting for transfers between devices, gather_pieces(): lax.ppermute(held, 'tile', [(b, b ^ mask) for b in range(count_tile)])  6.67 us
    ppermute x1, waiting for transfers between devices, gather_pieces(): other = lax.ppermute(held, ('len', 'tile'), pairs)  3.12 us
    ppermute x3, starting transfers between devices, gather_pieces(): lax.ppermute(held, 'tile', [(b, b ^ mask) for b in range(count_tile)])  3.11 us
    ppermute x1, waiting for transfers between devices, shards(): lax.ppermute(local, 'len', [(a, a ^ 1) for a in range(count_len)])  2.47 us
    ppermute x1, starting transfers between devices, shards(): lax.ppermute(local, 'len', [(a, a ^ 1) for a in range(count_len)])  1.48 us
    ppermute x1, starting transfers between devices, gather_pieces(): other = lax.ppermute(held, ('len', 'tile'), pairs)  1.43 us
  transfers between devices with their start and end apart: 5, of which 5 were waited for; matrix products, arithmetic and copies ran while one was open for 0% of the time, Pallas kernels for 0%

profile of v1, /device:TPU:12, one launch (start us, length us, event | category | flops | bytes accessed | tf_op | source)
XLA Modules:
  0.0 50.1 jit_solution(6223683879472320037)
XLA Ops:
  0.6 0.0 copy-start.3
  0.6 0.0 copy-start.2
  0.6 0.7 %convert_element_type.15 = f32[2]{0:T(128)S(1)} convert(s32[2]{0:T(128)} %param.5) | non-fusion elementwise | flops 2 | bytes 16 | tf_op jit(solution)/shard_map/convert_element_type | solution.py:34
  1.3 0.0 copy-done.3
  1.3 0.7 %convert_bitcast_fusion = f32[2,4]{1,0:T(2,128)S(1)} fusion(s32[4,2]{0,1:T(2,128)} %param.7), kind=kLoop, calls=%fused_computation.12 | loop fusion | flops 8 | bytes 64 | tf_op jit(solution)/shard_map/transpose | solution.py:28
  2.0 0.0 copy-done.2
  2.0 0.1 fusion.4
  2.1 0.1 collective-permute-start
  2.2 1.2 %collective-permute-done = f32[1,8,128]{2,1,0:T(8,128)S(1)} collective-permute-done((f32[1,8,128]{2,1,0:T(8,128)S(1)}, f32[1,8,128]{2,1,0:T(8,128)S(1)}, u32[]{:S(2)}, u32[]{:S(2)}) %collective-permute-start) | collective-permute-done | bytes 4128 | tf_op jit(solution)/shard_map/ppermute | solution.py:54
  3.3 1.4 %collective-permute-start.1 = (f32[2,8,128]{2,1,0:T(8,128)S(1)}, f32[2,8,128]{2,1,0:T(8,128)S(1)}, u32[]{:S(2)}, u32[]{:S(2)}) collective-permute-start(f32[2,8,128]{2,1,0:T(8,128)S(1)} %pad_maximum_fusion.2), channel_id=1, source_target_pairs={{0,18},{1,19},{2,16},{3,17},{4,22},{5,23},{6,20},{7,21},{8,26},{9,... | collective-permute-start | bytes 24584 | tf_op jit(solution)/shard_map/ppermute | solution.py:52
  4.8 3.1 %collective-permute-done.1 = f32[2,8,128]{2,1,0:T(8,128)S(1)} collective-permute-done((f32[2,8,128]{2,1,0:T(8,128)S(1)}, f32[2,8,128]{2,1,0:T(8,128)S(1)}, u32[]{:S(2)}, u32[]{:S(2)}) %collective-permute-start.1) | collective-permute-done | bytes 8224 | tf_op jit(solution)/shard_map/ppermute | solution.py:52
  7.9 0.4 collective-permute-start.2
  8.3 3.3 %collective-permute-done.2 = f32[4,8,128]{2,1,0:T(8,128)S(1)} collective-permute-done((f32[4,8,128]{2,1,0:T(8,128)S(1)}, f32[4,8,128]{2,1,0:T(8,128)S(1)}, u32[]{:S(2)}, u32[]{:S(2)}) %collective-permute-start.2) | collective-permute-done | bytes 16416 | tf_op jit(solution)/shard_map/ppermute | solution.py:54
  11.6 0.0 copy-start
  11.6 2.6 %collective-permute-start.3 = (f32[8,8,128]{2,1,0:T(8,128)S(1)}, f32[8,8,128]{2,1,0:T(8,128)S(1)}, u32[]{:S(2)}, u32[]{:S(2)}) collective-permute-start(f32[8,8,128]{2,1,0:T(8,128)S(1)} %pad_maximum_fusion.first_ref), channel_id=1, source_target_pairs={{0,8},{1,9},{2,10},{3,11},{4,12},{5,13},{6,14},{7,15},{8,0},{9,1},... | collective-permute-start | bytes 98312 | tf_op jit(solution)/shard_map/ppermute | solution.py:54
  14.2 2.2 %collective-permute-done.3.second_ref = f32[8,8,128]{2,1,0:T(8,128)S(1)} collective-permute-done((f32[8,8,128]{2,1,0:T(8,128)S(1)}, f32[8,8,128]{2,1,0:T(8,128)S(1)}, u32[]{:S(2)}, u32[]{:S(2)}) %collective-permute-start.3) | collective-permute-done | bytes 32800 | tf_op jit(solution)/shard_map/ppermute | solution.py:54
  16.5 0.0 copy-done
  16.5 0.0 copy-start.1
  16.5 0.6 %copy-done.1 = f32[8,8,128]{2,1,0:T(8,128)} copy-done((f32[8,8,128]{2,1,0:T(8,128)}, f32[8,8,128]{2,1,0:T(8,128)S(1)}, u32[]{:S(2)}) %copy-start.1) | copy-done | bytes 32792
  17.1 27.8 %profiles.1 = f32[8,512]{1,0:T(8,128)} custom-call(f32[8,8,128]{2,1,0:T(8,128)} %copy-done, f32[8,8,128]{2,1,0:T(8,128)} %copy-done.1), custom_call_target="tpu_custom_call" | custom-call | tf_op jit(solution)/shard_map/profiles/pallas_call | solution.py:276
  44.8 1.5 %collective-permute-start.4 = (f32[8,512]{1,0:T(8,128)}, f32[8,512]{1,0:T(8,128)S(1)}, u32[]{:S(2)}, u32[]{:S(2)}) collective-permute-start(f32[8,512]{1,0:T(8,128)} %profiles.1), channel_id=1, source_target_pairs={{0,16},{16,0},{1,17},{17,1},{2,18},{18,2},{3,19},{19,3},{4,20},{20... | collective-permute-start | bytes 49160 | tf_op jit(solution)/shard_map/ppermute | solution.py:305
  46.3 2.5 %collective-permute-done.4 = f32[8,512]{1,0:T(8,128)S(1)} collective-permute-done((f32[8,512]{1,0:T(8,128)}, f32[8,512]{1,0:T(8,128)S(1)}, u32[]{:S(2)}, u32[]{:S(2)}) %collective-permute-start.4) | collective-permute-done | bytes 16416 | tf_op jit(solution)/shard_map/ppermute | solution.py:305
  48.8 0.7 %min.3 = f32[8,512]{1,0:T(8,128)S(1)} minimum(f32[8,512]{1,0:T(8,128)} %profiles.1, f32[8,512]{1,0:T(8,128)S(1)} %collective-permute-done.4) | non-fusion elementwise | flops 4096 | bytes 49152 | tf_op jit(solution)/shard_map/min | solution.py:305
  49.5 0.6 %fusion.5 = (f32[4,512]{1,0:T(4,128)}, f32[4,512]{1,0:T(4,128)}) fusion(f32[8,512]{1,0:T(8,128)S(1)} %min.3), kind=kLoop, calls=%fused_computation.15 | loop fusion | bytes 32768 | tf_op jit(solution)/shard_map/slice | solution.py:310
  (6 shorter events, 0.0 us)
Async XLA Ops:
  0.6 0.7 %copy-start.3 = (s32[2]{0:T(128)S(1)}, s32[2]{0:T(128)}, u32[]{:S(2)}) copy-start(s32[2]{0:T(128)} %param.6) | copy-start | bytes 28
  0.6 1.4 %copy-start.2 = (f32[576]{0:T(1024)S(1)}, f32[576]{0:T(1024)}, u32[]{:S(2)}) copy-start(f32[576]{0:T(1024)} %param.4) | copy-start | bytes 6916
  2.1 1.2 %collective-permute-start = (f32[1,8,128]{2,1,0:T(8,128)S(1)}, f32[1,8,128]{2,1,0:T(8,128)S(1)}, u32[]{:S(2)}, u32[]{:S(2)}) collective-permute-start(f32[1,8,128]{2,1,0:T(8,128)S(1)} %fusion.1), channel_id=1, source_target_pairs={{0,1},{1,0},{2,3},{3,2},{4,5},{5,4},{6,7},{7,6},{8,9},{9,8},{10,11... | collective-permute-start | bytes 12296 | tf_op jit(solution)/shard_map/ppermute | solution.py:54
  3.3 4.5 %collective-permute-start.1 = (f32[2,8,128]{2,1,0:T(8,128)S(1)}, f32[2,8,128]{2,1,0:T(8,128)S(1)}, u32[]{:S(2)}, u32[]{:S(2)}) collective-permute-start(f32[2,8,128]{2,1,0:T(8,128)S(1)} %pad_maximum_fusion.2), channel_id=1, source_target_pairs={{0,18},{1,19},{2,16},{3,17},{4,22},{5,23},{6,20},{7,21},{8,26},{9,... | collective-permute-start | bytes 24584 | tf_op jit(solution)/shard_map/ppermute | solution.py:52
  7.9 3.7 %collective-permute-start.2 = (f32[4,8,128]{2,1,0:T(8,128)S(1)}, f32[4,8,128]{2,1,0:T(8,128)S(1)}, u32[]{:S(2)}, u32[]{:S(2)}) collective-permute-start(f32[4,8,128]{2,1,0:T(8,128)S(1)} %pad_maximum_fusion.1), channel_id=1, source_target_pairs={{0,4},{1,5},{2,6},{3,7},{4,0},{5,1},{6,2},{7,3},{8,12},{9,13},{10,... | collective-permute-start | bytes 49160 | tf_op jit(solution)/shard_map/ppermute | solution.py:54
  11.6 4.8 %copy-start = (f32[8,8,128]{2,1,0:T(8,128)}, f32[8,8,128]{2,1,0:T(8,128)S(1)}, u32[]{:S(2)}) copy-start(f32[8,8,128]{2,1,0:T(8,128)S(1)} %pad_maximum_fusion.first_ref) | copy-start | bytes 98308
  11.6 4.8 %collective-permute-start.3 = (f32[8,8,128]{2,1,0:T(8,128)S(1)}, f32[8,8,128]{2,1,0:T(8,128)S(1)}, u32[]{:S(2)}, u32[]{:S(2)}) collective-permute-start(f32[8,8,128]{2,1,0:T(8,128)S(1)} %pad_maximum_fusion.first_ref), channel_id=1, source_target_pairs={{0,8},{1,9},{2,10},{3,11},{4,12},{5,13},{6,14},{7,15},{8,0},{9,1},... | collective-permute-start | bytes 98312 | tf_op jit(solution)/shard_map/ppermute | solution.py:54
  16.5 0.6 %copy-start.1 = (f32[8,8,128]{2,1,0:T(8,128)}, f32[8,8,128]{2,1,0:T(8,128)S(1)}, u32[]{:S(2)}) copy-start(f32[8,8,128]{2,1,0:T(8,128)S(1)} %collective-permute-done.3.second_ref) | copy-start | bytes 98308
  44.8 3.9 %collective-permute-start.4 = (f32[8,512]{1,0:T(8,128)}, f32[8,512]{1,0:T(8,128)S(1)}, u32[]{:S(2)}, u32[]{:S(2)}) collective-permute-start(f32[8,512]{1,0:T(8,128)} %profiles.1), channel_id=1, source_target_pairs={{0,16},{16,0},{1,17},{17,1},{2,18},{18,2},{3,19},{19,3},{4,20},{20... | collective-permute-start | bytes 49160 | tf_op jit(solution)/shard_map/ppermute | solution.py:305
